TPU v7x, 32 devices: a whole 2x2x4 slice. The times are simulated.
32 devices in a mesh: gx: 8 (over y, x, core), gy: 4 (over z).
Axes of the slice: x: 2, y: 2, z: 4, core: 2. Of those that a mesh axis runs over, the one named last changes fastest.
Arguments:
- positions: float32 [3, 4096], P(None, ('gx', 'gy')), may hold values from 0 to 1
- species: int32 [4096], P(('gx', 'gy')), may hold values from 0 to 3
- neighbours: int32 [8, 4096], P(None, ('gx', 'gy')), may hold values from 0 to 639, as said below
- counts: int32 [4096], P(('gx', 'gy')), may hold values from 0 to 8, as said below
- live_atoms: int32 [32], P(('gx', 'gy')), may hold values from 64 to 128, as said below
- ghost_send: int32 [16384], P(('gx', 'gy')), may hold values from 0 to 127, as said below
- embed: float32 [128, 4], replicated, may hold values from -6 to 6
- site_energy: float32 [4], replicated, may hold values from -6 to 6
- radial_in: float32 [2, 64, 8], replicated, may hold values from -3 to 3
- radial_mid: float32 [2, 64, 64], replicated, may hold values from -1 to 1
- radial_out: float32 [2, 384, 64], replicated, may hold values from -1.5 to 1.5
- contract: float32 [2, 4, 6, 128], replicated, may hold values from -6 to 6
- mix: float32 [2, 128, 128], replicated, may hold values from -1 to 1
- skip: float32 [2, 128, 128], replicated, may hold values from -0.5 to 0.5
- read_one: float32 [128], replicated, may hold values from -1 to 1
- read_hidden: float32 [16, 128], replicated, may hold values from -1 to 1
- read_out: float32 [16], replicated, may hold values from -3 to 3
Outputs:
- energy: float32 [], replicated
- forces: float32 [3, 4096], P(None, ('gx', 'gy'))
- stress: float32 [3, 3], replicated
Inputs may be any that keep to these rules, and one draw needn't show every extreme that they name: `live_atoms`: device 0 holds 128 real atoms. `counts`: zero for padding atoms; atom slot 0 of every device uses all 8 slots. `neighbours`: the used slots of an atom name a real atom of the same device (below its live count) or a ghost slot, numbered from 128 in the order of directions. `ghost_send`: each entry names a real atom of the sending device.
All inputs are finite; a program needn't handle non-finite values.
Results may differ from a plain program's by a relative error of at most 0.0003.
Values sent between devices are 32-bit elements; how exact they have to be, the bound alone decides.
A program may use at most 64 MiB of HBM per device.

v0:
```python
import functools

import jax
import jax.numpy as jnp
from jax import lax
from jax.experimental import pallas as pl
from jax.experimental.pallas import tpu as pltpu
from jax.sharding import PartitionSpec as P

f32 = jnp.float32
bf16 = jnp.bfloat16
MESH = pl.DeviceIdType.MESH
cut_sq = 4.0
span = 2.0
directions = ((-1, -1), (-1, 0), (-1, 1), (0, -1), (0, 1), (1, -1), (1, 0), (1, 1))
BLOCK = 16


def dot(a, b):
    return lax.dot_general(a, b, (((1,), (0,)), ((), ())), preferred_element_type=f32)


def dot_nt(a, b):
    return lax.dot_general(a, b, (((1,), (1,)), ((), ())), preferred_element_type=f32)


def halves(x):
    high = x.astype(bf16)
    return high, (x - high.astype(f32)).astype(bf16)


def stacked(x, parts):
    terms = []
    rest = x
    for _ in range(parts - 1):
        term = rest.astype(bf16).astype(f32)
        terms.append(term)
        rest = rest - term
    terms.append(rest)
    if (parts * x.shape[0]) % 16:
        terms.append(jnp.zeros_like(x))
    return jnp.concatenate(terms, 0).astype(bf16)


def unstacked(y, rows, parts):
    total = y[(parts - 1) * rows : parts * rows]
    for at in range(parts - 2, -1, -1):
        total = total + y[at * rows : (at + 1) * rows]
    return total


def dot3(a, b):
    a_high, a_low = halves(a)
    b_high, b_low = halves(b)
    return dot(a_high, b_high) + (dot(a_high, b_low) + dot(a_low, b_high))


def sub_iota(shape):
    return lax.broadcasted_iota(jnp.int32, shape, 0)


def lane_iota(shape):
    return lax.broadcasted_iota(jnp.int32, shape, 1)


def kernel(
    n_gx,
    n_gy,
    pos_ref,
    kind_ref,
    neigh_ref,
    count_ref,
    live_ref,
    send_ref,
    embed_ref,
    site_ref,
    win_ref,
    wmid_ref,
    wout_ref,
    contract_ref,
    mix_ref,
    skip_ref,
    one_ref,
    hidden_ref,
    out_ref,
    energy_ref,
    forces_ref,
    stress_ref,
    packet,
    table,
    embed_pad,
    place,
    place_back,
    pick,
    rows,
    grads,
    sel,
    rad0,
    drad0,
    rad1,
    drad1,
    feat0,
    feat1,
    deriv0,
    deriv1,
    mixed,
    first,
    gmix,
    gfeat,
    zed,
    gown,
    p_send,
    p_recv,
    f_send,
    f_recv,
    g_send,
    g_recv,
    q_send,
    q_recv,
    y_recv,
    x_send,
    x_recv,
    p_ss,
    p_rs,
    f_ss,
    f_rs,
    g_ss,
    g_rs,
    q_ss,
    q_rs,
    y_ss,
    y_rs,
    x_ss,
    x_rs,
):
    channels = embed_ref.shape[0]
    kinds = embed_ref.shape[1]
    slots, atoms = neigh_ref.shape
    edges = slots * atoms
    ghosts = send_ref.shape[1]
    ghost = ghosts // 8
    basis_count = win_ref.shape[2]
    hid = win_ref.shape[1]
    me_x = lax.axis_index("gx")
    me_y = lax.axis_index("gy")

    def at(off_x, off_y):
        return {
            "gx": lax.rem(me_x + (off_x + n_gx), n_gx),
            "gy": lax.rem(me_y + (off_y + n_gy), n_gy),
        }

    barrier = pltpu.get_barrier_semaphore()
    friends = [(ox, oy) for ox, oy in directions if ox and oy]
    friends += [(t, 0) for t in range(1, n_gx)] + [(0, t) for t in range(1, n_gy)]
    for ox, oy in friends:
        pl.semaphore_signal(barrier, inc=1, device_id=at(ox, oy), device_id_type=MESH)

    kind = kind_ref[...]
    packet[...] = jnp.zeros_like(packet)
    packet[0:3, :] = pos_ref[...]
    packet[3:4, :] = kind.astype(f32)
    own = packet[...]
    place_f = (sub_iota((atoms, ghosts)) == send_ref[...]).astype(f32)
    place[...] = place_f.astype(bf16)
    sent = unstacked(dot(stacked(own, 3), place[...]), 8, 3)
    for pair in range(4):
        p_send[pair] = sent[:, pair * 2 * ghost : (pair + 1) * 2 * ghost]

    def ghost_copy(src, dst, ss, rs, heading, sign):
        ox, oy = directions[heading]
        return pltpu.make_async_remote_copy(
            src_ref=src,
            dst_ref=dst,
            send_sem=ss.at[heading],
            recv_sem=rs.at[heading],
            device_id=at(sign * ox, sign * oy),
            device_id_type=MESH,
        )

    pl.semaphore_wait(barrier, len(friends))
    p_copies = [
        ghost_copy(p_send.at[d // 2], p_recv.at[d], p_ss, p_rs, d, -1) for d in range(8)
    ]
    for copy in p_copies:
        copy.start()

    for k in range(slots):
        pick[:, k * atoms : (k + 1) * atoms] = (
            (sub_iota((atoms + ghosts, atoms)) == neigh_ref[k : k + 1, :])
            .astype(f32)
            .astype(bf16)
        )
    for b in range(ghosts // atoms):
        place_back[b * atoms : (b + 1) * atoms, :] = jnp.transpose(
            place_f[:, b * atoms : (b + 1) * atoms]
        ).astype(bf16)
    table[...] = jnp.zeros_like(table)
    for layer in range(2):
        for s in range(kinds):
            base = (layer * kinds + s) * 8
            table[base : base + 6, :] = contract_ref[layer, s]
    table_high, table_low = halves(jnp.transpose(table[...]))
    for layer in range(2):
        for p in range(6):
            chosen = (
                (sub_iota((channels, atoms)) == kind * 8 + (layer * kinds * 8 + p))
                .astype(f32)
                .astype(bf16)
            )
            sel[layer, p] = dot(table_high, chosen) + dot(table_low, chosen)
    embed_pad[...] = jnp.zeros_like(embed_pad)
    embed_pad[:, 0:kinds] = embed_ref[...]
    embed_stack = stacked(embed_pad[...], 2)
    kind_local = (sub_iota((channels, atoms)) == kind).astype(f32).astype(bf16)
    start_self = unstacked(dot(embed_stack, kind_local), channels, 2)
    skip_part = dot3(skip_ref[0], start_self)
    read_mix = dot3(hidden_ref[...], mix_ref[1])
    read_skip = dot3(hidden_ref[...], skip_ref[1])
    live = (lane_iota((1, atoms)) < live_ref[0]).astype(f32)
    one_full = jnp.transpose(jnp.broadcast_to(one_ref[...], (atoms, channels)))
    readers = hidden_ref.shape[0]
    out_column = jnp.sum(
        jnp.where(
            sub_iota((readers, readers)) == lane_iota((readers, readers)), out_ref[...], 0.0
        ),
        axis=1,
        keepdims=True,
    )
    mix_back_high, mix_back_low = halves(jnp.transpose(mix_ref[0]))

    tiles = [own]
    lane = lane_iota((8, 2 * ghost))
    sub = sub_iota((8, 2 * ghost))
    for copy in p_copies:
        copy.wait_recv()
    for pair in range(4):
        (ax, ay), (bx, by) = directions[2 * pair], directions[2 * pair + 1]
        tile = jnp.where(lane < ghost, p_recv[2 * pair], p_recv[2 * pair + 1])
        off_x = jnp.where(lane < ghost, float(ax), float(bx))
        off_y = jnp.where(lane < ghost, float(ay), float(by))
        tiles.append(tile + jnp.where(sub == 0, off_x, jnp.where(sub == 1, off_y, 0.0)))
    ext = stacked(jnp.concatenate(tiles, 1), 3)
    rows[0:8, :] = unstacked(dot(ext, pick[...]), 8, 3)
    kind_edge = (
        (sub_iota((channels, edges)).astype(f32) == rows[3:4, :]).astype(f32).astype(bf16)
    )
    feat0[...] = unstacked(dot(embed_stack, kind_edge), channels, 2)
    for k in range(slots):
        lanes = slice(k * atoms, (k + 1) * atoms)
        x = rows[0:1, lanes] - pos_ref[0:1, :]
        y = rows[1:2, lanes] - pos_ref[1:2, :]
        z = rows[2:3, lanes] - pos_ref[2:3, :]
        rows[0:1, lanes] = x
        rows[1:2, lanes] = y
        rows[2:3, lanes] = z
        rows[3:4, lanes] = x * y
        rows[4:5, lanes] = y * z
        rows[5:6, lanes] = x * z
        rows[6:7, lanes] = 0.5 * (x * x - y * y)
        rows[7:8, lanes] = (2.0 * z * z - x * x - y * y) / 6.0
        squared = (x * x + y * y + z * z) / cut_sq
        rows[8:9, lanes] = squared
        valid = (count_ref[...] > k).astype(f32)
        rows[9:10, lanes] = jnp.exp(-squared) * valid * (1.0 / slots)

    spacing = span / (basis_count - 1)
    scaled = jnp.broadcast_to(rows[8:9, :], (basis_count, edges))
    gap = (scaled - sub_iota((basis_count, edges)).astype(f32) * spacing) / spacing
    basis = jnp.exp(-0.5 * gap * gap)
    basis_all = jnp.concatenate([basis, basis * gap * (-1.0 / spacing)], 1)

    def deep(w, x):
        w_high, w_low = halves(w)
        w_high, w_low = w_high.astype(f32), w_low.astype(f32)
        x_high = x.astype(bf16).astype(f32)
        left = jnp.concatenate([w_high, w_high, w_low], 1).astype(bf16)
        right = jnp.concatenate([x_high, x - x_high, x_high], 0).astype(bf16)
        return dot(left, right)

    def silu_pair(z):
        value, slope = z[:, :edges], z[:, edges:]
        gate = 1.0 / (1.0 + jnp.exp(-value))
        act = value * gate
        return act, (gate + act * (1.0 - gate)) * slope

    def network(layer):
        h, dh = silu_pair(deep(win_ref[layer], basis_all))
        h, dh = silu_pair(deep(wmid_ref[layer], jnp.concatenate([h, dh], 1)))
        env = rows[9:10, :]
        return h * env, (dh - h) * env

    def moments(layer, rad, feat, deriv):
        def step(block, carry):
            base = pl.multiple_of(block * BLOCK, BLOCK)
            here = pl.ds(base, BLOCK)
            acc = [jnp.zeros((BLOCK, atoms), f32) for _ in range(9)]
            for k in range(slots):
                lanes = slice(k * atoms, (k + 1) * atoms)
                h = feat[here, lanes]
                acc[0] = acc[0] + rad[pl.ds(base, BLOCK), lanes] * h
                w1 = rad[pl.ds(base + channels, BLOCK), lanes] * h
                w2 = rad[pl.ds(base + 2 * channels, BLOCK), lanes] * h
                for m in range(3):
                    acc[1 + m] = acc[1 + m] + w1 * rows[m : m + 1, lanes]
                for m in range(5):
                    acc[4 + m] = acc[4 + m] + w2 * rows[3 + m : 4 + m, lanes]
            a0, v0, v1, v2, xy, yz, xz, u, w = acc
            c0, c1, c2, c3, c4, c5 = [sel[layer, p, here, :] for p in range(6)]
            q1 = v0 * v0 + v1 * v1 + v2 * v2
            q2 = xy * xy + yz * yz + xz * xz + u * u + w * w
            m0 = (u - w) * v0 + xy * v1 + xz * v2
            m1 = xy * v0 - (u + w) * v1 + yz * v2
            m2 = xz * v0 + yz * v1 + 2.0 * w * v2
            triple = v0 * m0 + v1 * m1 + v2 * m2
            d1 = c2 + c4 * a0
            mixed[here, :] = (c0 + c1 * a0) * a0 + d1 * q1 + c3 * q2 + c5 * triple
            deriv[0, here, :] = c0 + 2.0 * c1 * a0 + c4 * q1
            deriv[1, here, :] = 2.0 * (d1 * v0 + c5 * m0)
            deriv[2, here, :] = 2.0 * (d1 * v1 + c5 * m1)
            deriv[3, here, :] = 2.0 * (d1 * v2 + c5 * m2)
            deriv[4, here, :] = 2.0 * (c3 * xy + c5 * (v0 * v1))
            deriv[5, here, :] = 2.0 * (c3 * yz + c5 * (v1 * v2))
            deriv[6, here, :] = 2.0 * (c3 * xz + c5 * (v0 * v2))
            deriv[7, here, :] = 2.0 * c3 * u + c5 * (v0 * v0 - v1 * v1)
            deriv[8, here, :] = 2.0 * c3 * w + c5 * (2.0 * v2 * v2 - v0 * v0 - v1 * v1)
            return carry

        lax.fori_loop(0, channels // BLOCK, step, 0)

    act0, slope0 = network(0)
    rad0[...] = deep(wout_ref[0], act0)
    moments(0, rad0, feat0, deriv0)
    first[...] = dot3(mix_ref[0], mixed[...]) + skip_part
    first_high, first_low = halves(first[...])
    sent_first = dot_nt(place_back[...], first_high) + dot_nt(place_back[...], first_low)
    for d in range(8):
        f_send[d] = sent_first[d * ghost : (d + 1) * ghost]
    f_copies = [ghost_copy(f_send.at[d], f_recv.at[d], f_ss, f_rs, d, -1) for d in range(8)]
    for copy in f_copies:
        copy.start()
    for copy in p_copies:
        copy.wait_send()

    act1, slope1 = network(1)
    rad1[...] = deep(wout_ref[1], act1)
    drad0[...] = deep(wout_ref[0], slope0)
    drad1[...] = deep(wout_ref[1], slope1)

    for copy in f_copies:
        copy.wait_recv()
    arrived = f_recv[...].reshape(ghosts, channels)
    turned = [first[...]] + [
        jnp.transpose(arrived[b * atoms : (b + 1) * atoms]) for b in range(ghosts // atoms)
    ]
    ext_first = stacked(jnp.concatenate(turned, 1), 2)
    feat1[...] = unstacked(dot(ext_first, pick[...]), channels, 2)
    moments(1, rad1, feat1, deriv1)
    inner = dot3(read_mix, mixed[...]) + dot3(read_skip, first[...])
    gate = 1.0 / (1.0 + jnp.exp(-inner))
    act = inner * gate
    g_inner = (gate + act * (1.0 - gate)) * out_column * live
    gmix[...] = dot3(jnp.transpose(read_mix), g_inner)

    def feature_grad(block, carry):
        base = pl.multiple_of(block * BLOCK, BLOCK)
        here = pl.ds(base, BLOCK)
        g = gmix[here, :]
        ga = [g * deriv1[m, here, :] for m in range(9)]
        for k in range(slots):
            lanes = slice(k * atoms, (k + 1) * atoms)
            t1 = sum(ga[1 + m] * rows[m : m + 1, lanes] for m in range(3))
            t2 = sum(ga[4 + m] * rows[3 + m : 4 + m, lanes] for m in range(5))
            total = ga[0] * rad1[pl.ds(base, BLOCK), lanes]
            total = total + t1 * rad1[pl.ds(base + channels, BLOCK), lanes]
            total = total + t2 * rad1[pl.ds(base + 2 * channels, BLOCK), lanes]
            high = total.astype(bf16)
            gfeat[pl.ds(base, BLOCK), lanes] = high
            gfeat[pl.ds(base + channels, BLOCK), lanes] = (total - high.astype(f32)).astype(bf16)
        return carry

    lax.fori_loop(0, channels // BLOCK, feature_grad, 0)
    back = dot_nt(pick[atoms : atoms + ghosts, :], gfeat[...])
    back = back[:, :channels] + back[:, channels:]
    for d in range(8):
        g_send[d] = back[d * ghost : (d + 1) * ghost]
    g_copies = [ghost_copy(g_send.at[d], g_recv.at[d], g_ss, g_rs, d, 1) for d in range(8)]
    for copy in g_copies:
        copy.start()
    for copy in f_copies:
        copy.wait_send()

    own_back = dot_nt(pick[0:atoms, :], gfeat[...])
    own_back = jnp.transpose(own_back[:, :channels] + own_back[:, channels:])
    gown[...] = own_back + dot3(jnp.transpose(read_skip), g_inner) + one_full * live
    energy_lanes = live * jnp.sum(one_full * first[...], axis=0, keepdims=True)
    energy_lanes = energy_lanes + live * jnp.sum(out_column * act, axis=0, keepdims=True)
    for s in range(kinds):
        energy_lanes = energy_lanes + jnp.where(kind == s, site_ref[s], 0.0) * live

    def edge_terms(rad, drad, feat, deriv, base, lanes):
        here = pl.ds(base, BLOCK)
        x, y, z = [rows[m : m + 1, lanes] for m in range(3)]
        h = feat[here, lanes]
        dv = [deriv[m, here, :] for m in range(9)]
        t1 = sum(dv[1 + m] * rows[m : m + 1, lanes] for m in range(3))
        t2 = sum(dv[4 + m] * rows[3 + m : 4 + m, lanes] for m in range(5))
        ds = dv[0] * drad[pl.ds(base, BLOCK), lanes]
        ds = ds + t1 * drad[pl.ds(base + channels, BLOCK), lanes]
        ds = ds + t2 * drad[pl.ds(base + 2 * channels, BLOCK), lanes]
        ds = ds * (2.0 / cut_sq)
        r1 = rad[pl.ds(base + channels, BLOCK), lanes]
        r2 = rad[pl.ds(base + 2 * channels, BLOCK), lanes]
        third = dv[8] * (1.0 / 3.0)
        gx = ds * x + r1 * dv[1] + r2 * (dv[4] * y + dv[6] * z + (dv[7] - third) * x)
        gy = ds * y + r1 * dv[2] + r2 * (dv[4] * x + dv[5] * z - (dv[7] + third) * y)
        gz = ds * z + r1 * dv[3] + r2 * (dv[5] * y + dv[6] * x + (2.0 * third) * z)
        return h * gx, h * gy, h * gz

    def first_terms(block, carry):
        base = pl.multiple_of(block * BLOCK, BLOCK)
        for k in range(slots):
            lanes = slice(k * atoms, (k + 1) * atoms)
            terms = edge_terms(rad0, drad0, feat0, deriv0, base, lanes)
            for i in range(3):
                zed[i, pl.ds(base, BLOCK), lanes] = terms[i]
        return carry

    lax.fori_loop(0, channels // BLOCK, first_terms, 0)
    for k in range(slots):
        lanes = slice(k * atoms, (k + 1) * atoms)

        def second_terms(block, carry):
            base = pl.multiple_of(block * BLOCK, BLOCK)
            terms = edge_terms(rad1, drad1, feat1, deriv1, base, lanes)
            g = gmix[pl.ds(base, BLOCK), :]
            return tuple(carry[i] + g * terms[i] for i in range(3))

        zero = jnp.zeros((BLOCK, atoms), f32)
        sums = lax.fori_loop(0, channels // BLOCK, second_terms, (zero, zero, zero))
        for i in range(3):
            grads[i : i + 1, lanes] = jnp.sum(sums[i], axis=0, keepdims=True)

    for copy in g_copies:
        copy.wait_recv()
    returned = g_recv[...].reshape(ghosts, channels)
    turned = jnp.concatenate(
        [jnp.transpose(returned[b * atoms : (b + 1) * atoms]) for b in range(ghosts // atoms)], 1
    )
    home = unstacked(dot(stacked(turned, 2), place_back[...]), channels, 2)
    g_high, g_low = halves(gown[...] + home)
    gmix[...] = (
        dot(mix_back_high, g_high) + dot(mix_back_high, g_low) + dot(mix_back_low, g_high)
    )
    for k in range(slots):
        lanes = slice(k * atoms, (k + 1) * atoms)
        for i in range(3):
            grads[i : i + 1, lanes] = grads[i : i + 1, lanes] + jnp.sum(
                gmix[...] * zed[i, :, lanes], axis=0, keepdims=True
            )
    for copy in g_copies:
        copy.wait_send()
    grads[3:8, :] = jnp.zeros((5, edges), f32)
    ext_grad = unstacked(dot_nt(stacked(grads[...], 2), pick[...]), 8, 2)
    for pair in range(4):
        q_send[pair] = ext_grad[:, atoms + pair * 2 * ghost : atoms + (pair + 1) * 2 * ghost]
    q_copies = [
        ghost_copy(q_send.at[d // 2], q_recv.at[d], q_ss, q_rs, d, 1) for d in range(8)
    ]
    for copy in q_copies:
        copy.start()

    partial = [energy_lanes, live]
    for a in range(3):
        for b in range(3):
            total = jnp.zeros((1, atoms), f32)
            for k in range(slots):
                lanes = slice(k * atoms, (k + 1) * atoms)
                total = total + rows[a : a + 1, lanes] * grads[b : b + 1, lanes]
            partial.append(total)
    partial.append(jnp.zeros((5, atoms), f32))
    y_recv[me_y] = jnp.concatenate(partial, 0)

    def line_copies(buf, ss, rs, me, count, where):
        outgoing = []
        incoming = []
        for t in range(1, count):
            source = lax.rem(me + (count - t), count)
            outgoing.append(
                pltpu.make_async_remote_copy(
                    src_ref=buf.at[me],
                    dst_ref=buf.at[me],
                    send_sem=ss.at[t],
                    recv_sem=rs.at[t],
                    device_id=where(t),
                    device_id_type=MESH,
                )
            )
            incoming.append(
                pltpu.make_async_remote_copy(
                    src_ref=buf.at[source],
                    dst_ref=buf.at[source],
                    send_sem=ss.at[t],
                    recv_sem=rs.at[t],
                    device_id=where(t),
                    device_id_type=MESH,
                )
            )
        return outgoing, incoming

    y_out, y_in = line_copies(y_recv, y_ss, y_rs, me_y, n_gy, lambda t: at(0, t))
    for copy in y_out:
        copy.start()
    own_grad = ext_grad[:, :atoms]
    for k in range(slots):
        own_grad = own_grad - grads[:, k * atoms : (k + 1) * atoms]
    for copy in y_in:
        copy.wait_recv()
    total = y_recv[0]
    for t in range(1, n_gy):
        total = total + y_recv[t]
    x_recv[me_x] = total
    x_out, x_in = line_copies(x_recv, x_ss, x_rs, me_x, n_gx, lambda t: at(t, 0))
    for copy in x_out:
        copy.start()

    for copy in q_copies:
        copy.wait_recv()
    tiles = [
        jnp.where(lane < ghost, q_recv[2 * pair], q_recv[2 * pair + 1]) for pair in range(4)
    ]
    home_pos = unstacked(dot(stacked(jnp.concatenate(tiles, 1), 2), place_back[...]), 8, 2)
    forces_ref[...] = -(own_grad + home_pos)[0:3]

    for copy in x_in:
        copy.wait_recv()
    total = x_recv[0]
    for t in range(1, n_gx):
        total = total + x_recv[t]
    total = jnp.sum(total, axis=1, keepdims=True)
    scaled_total = total / total[1:2]
    energy_ref[...] = scaled_total[0:1]
    corner_r, corner_c = sub_iota((3, 3)), lane_iota((3, 3))
    stress = jnp.zeros((3, 3), f32)
    for a in range(3):
        for b in range(3):
            value = scaled_total[2 + 3 * a + b : 3 + 3 * a + b]
            stress = jnp.where((corner_r == a) & (corner_c == b), value, stress)
    stress_ref[...] = stress
    for copy in q_copies + y_out + x_out:
        copy.wait_send()


def solution(mesh):
    n_gx, n_gy = mesh.shape["gx"], mesh.shape["gy"]

    def per_device(
        positions, species, neighbours, counts, live_atoms, ghost_send, embed, site_energy,
        radial_in, radial_mid, radial_out, contract, mix, skip, read_one, read_hidden, read_out,
    ):
        channels = embed.shape[0]
        slots, atoms = neighbours.shape
        edges = slots * atoms
        ghosts = ghost_send.shape[0]
        ghost = ghosts // 8
        vmem = pl.BlockSpec(memory_space=pltpu.VMEM)
        smem = pl.BlockSpec(memory_space=pltpu.SMEM)
        sems = pltpu.SemaphoreType.DMA
        wide = (channels, edges)
        scratch = [
            pltpu.VMEM((8, atoms), f32),
            pltpu.VMEM((channels, channels), f32),
            pltpu.VMEM((channels, channels), f32),
            pltpu.VMEM((atoms, ghosts), bf16),
            pltpu.VMEM((ghosts, atoms), bf16),
            pltpu.VMEM((atoms + ghosts, edges), bf16),
            pltpu.VMEM((16, edges), f32),
            pltpu.VMEM((8, edges), f32),
            pltpu.VMEM((2, 6, channels, atoms), f32),
            pltpu.VMEM((3 * channels, edges), f32),
            pltpu.VMEM((3 * channels, edges), f32),
            pltpu.VMEM((3 * channels, edges), f32),
            pltpu.VMEM((3 * channels, edges), f32),
            pltpu.VMEM(wide, f32),
            pltpu.VMEM(wide, f32),
            pltpu.VMEM((9, channels, atoms), f32),
            pltpu.VMEM((9, channels, atoms), f32),
            pltpu.VMEM((channels, atoms), f32),
            pltpu.VMEM((channels, atoms), f32),
            pltpu.VMEM((channels, atoms), f32),
            pltpu.VMEM((2 * channels, edges), bf16),
            pltpu.VMEM((3, channels, edges), f32),
            pltpu.VMEM((channels, atoms), f32),
            pltpu.VMEM((4, 8, 2 * ghost), f32),
            pltpu.VMEM((8, 8, 2 * ghost), f32),
            pltpu.VMEM((8, ghost, channels), f32),
            pltpu.VMEM((8, ghost, channels), f32),
            pltpu.VMEM((8, ghost, channels), f32),
            pltpu.VMEM((8, ghost, channels), f32),
            pltpu.VMEM((4, 8, 2 * ghost), f32),
            pltpu.VMEM((8, 8, 2 * ghost), f32),
            pltpu.VMEM((n_gy, 16, atoms), f32),
            pltpu.VMEM((16, atoms), f32),
            pltpu.VMEM((n_gx, 16, atoms), f32),
        ]
        scratch += [sems((8,))] * 8 + [sems((n_gy,))] * 2 + [sems((n_gx,))] * 2
        energy, forces, stress = pl.pallas_call(
            functools.partial(kernel, n_gx, n_gy),
            out_shape=(
                jax.ShapeDtypeStruct((1, 1), f32),
                jax.ShapeDtypeStruct((3, atoms), f32),
                jax.ShapeDtypeStruct((3, 3), f32),
            ),
            in_specs=[vmem] * 4 + [smem] + [vmem] * 2 + [smem] + [vmem] * 9,
            out_specs=(vmem, vmem, vmem),
            scratch_shapes=scratch,
            compiler_params=pltpu.CompilerParams(
                collective_id=0, has_side_effects=True, vmem_limit_bytes=50 * 1024 * 1024
            ),
        )(
            positions, species[None], neighbours, counts[None], live_atoms, ghost_send[None],
            embed, site_energy, radial_in, radial_mid, radial_out, contract, mix, skip,
            read_one[None], read_hidden, read_out[None],
        )
        return energy.reshape(()), forces, stress

    flat = P(("gx", "gy"))
    columns = P(None, ("gx", "gy"))
    return jax.shard_map(
        per_device,
        mesh=mesh,
        in_specs=(columns, flat, columns, flat, flat, flat) + (P(),) * 11,
        out_specs=(P(), columns, P()),
        check_vma=False,
    )
```

profile of v0, /device:TPU:0, one launch (start us, length us, event | category | flops | bytes accessed | tf_op | source)
XLA Modules:
  0.0 47.5 jit_solution(12777972546222130236)
XLA Ops:
  0.6 0.0 copy-start.12
  1.3 0.7 %copy.23.contract_ref = f32[2,4,6,128]{3,2,1,0:T(8,128)S(1)} copy(f32[2,4,6,128]{3,1,2,0:T(4,128)} %param.28) | data formatting | bytes 49152 | tf_op args[11]
  2.1 0.8 %copy.20.embed_ref = f32[128,4]{1,0:T(8,128)S(1)} copy(f32[128,4]{0,1:T(4,128)} %param.23) | data formatting | bytes 4096 | tf_op args[6]
  2.9 0.8 %copy.21.win_ref = f32[2,64,8]{2,1,0:T(8,128)S(1)} copy(f32[2,64,8]{1,2,0:T(8,128)} %param.25) | data formatting | bytes 8192 | tf_op args[8]
  3.7 0.0 copy-done.12
  3.7 0.0 copy-start
  3.7 0.0 copy-start.1
  3.7 0.0 copy-start.2
  3.7 0.0 copy-start.3
  3.7 0.0 copy-start.4
  3.7 0.0 copy-start.5
  3.7 0.0 copy-start.6
  3.7 0.0 copy-start.7
  3.8 0.0 copy-start.8
  3.8 0.0 copy-start.9
  3.8 0.0 copy-start.10
  3.8 0.0 copy-start.11
  3.8 0.2 copy.22.wout_ref
  4.0 0.6 %copy-done = f32[2,128,128]{2,1,0:T(8,128)S(1)} copy-done((f32[2,128,128]{2,1,0:T(8,128)S(1)}, f32[2,128,128]{2,1,0:T(8,128)}, u32[]{:S(2)}) %copy-start) | copy-done | bytes 131096
  4.6 0.1 copy-done.1
  4.6 0.0 copy-done.4
  4.7 39.9 %shard_map.184 = (f32[1,1]{1,0:T(1,128)}, f32[3,128]{1,0:T(4,128)S(1)}, f32[3,3]{1,0:T(4,128)S(1)}) custom-call(f32[3,128]{1,0:T(4,128)S(1)} %copy-done.5, s32[1,128]{1,0:T(1,128)S(1)} %bitcast.7, s32[8,128]{1,0:T(8,128)S(1)} %copy-done.4, s32[1,128]{1,0:T(1,128)S(1)} %bitcast.8, s32[1]{0:T(128)S(6)} %copy.27.live_ref, s32[1,512]{1,0:T(1,128)S(1)} %bitcast.6, ...), custom_call_target="tpu_custom_call" | custom-call | tf_op jit(solution)/shard_map/pallas_call | solution.py:607
  45.2 0.6 %copy.29 = f32[3,128]{1,0:T(4,128)} copy(f32[3,128]{1,0:T(4,128)S(1)} %get-tuple-element.13) | data formatting | bytes 3072
  45.8 0.6 %copy.30 = f32[3,3]{1,0:T(4,128)} copy(f32[3,3]{1,0:T(4,128)S(1)} %get-tuple-element.14) | data formatting | bytes 72
  (9 shorter events, 0.0 us)
Async XLA Ops:
  0.6 3.0 %copy-start.12 = (f32[2,384,64]{1,2,0:T(8,128)S(1)}, f32[2,384,64]{1,2,0:T(8,128)}, u32[]{:S(2)}) copy-start(f32[2,384,64]{1,2,0:T(8,128)} %param.27) | copy-start | bytes 589828
  3.7 0.9 %copy-start = (f32[2,128,128]{2,1,0:T(8,128)S(1)}, f32[2,128,128]{2,1,0:T(8,128)}, u32[]{:S(2)}) copy-start(f32[2,128,128]{2,1,0:T(8,128)} %mix_ref.1) | copy-start | bytes 393220
  3.7 1.0 %copy-start.1 = (f32[2,128,128]{2,1,0:T(8,128)S(1)}, f32[2,128,128]{2,1,0:T(8,128)}, u32[]{:S(2)}) copy-start(f32[2,128,128]{2,1,0:T(8,128)} %skip_ref.1) | copy-start | bytes 393220
  3.7 1.0 %copy-start.2 = (f32[2,64,64]{2,1,0:T(8,128)S(1)}, f32[2,64,64]{2,1,0:T(8,128)}, u32[]{:S(2)}) copy-start(f32[2,64,64]{2,1,0:T(8,128)} %wmid_ref.1) | copy-start | bytes 98308
  3.7 0.9 %copy-start.3 = (f32[16,128]{1,0:T(8,128)S(1)}, f32[16,128]{1,0:T(8,128)}, u32[]{:S(2)}) copy-start(f32[16,128]{1,0:T(8,128)} %hidden_ref.1) | copy-start | bytes 24580
  3.7 0.9 %copy-start.4 = (s32[8,128]{1,0:T(8,128)S(1)}, s32[8,128]{1,0:T(8,128)}, u32[]{:S(2)}) copy-start(s32[8,128]{1,0:T(8,128)} %neigh_ref.1) | copy-start | bytes 12292
  3.7 0.9 %copy-start.5 = (f32[3,128]{1,0:T(4,128)S(1)}, f32[3,128]{1,0:T(4,128)}, u32[]{:S(2)}) copy-start(f32[3,128]{1,0:T(4,128)} %pos_ref.1) | copy-start | bytes 4612
  3.7 0.9 %copy-start.6 = (s32[512]{0:T(512)S(1)}, s32[512]{0:T(512)}, u32[]{:S(2)}) copy-start(s32[512]{0:T(512)} %param.22) | copy-start | bytes 6148
  3.7 0.9 %copy-start.7 = (s32[128]{0:T(128)S(1)}, s32[128]{0:T(128)}, u32[]{:S(2)}) copy-start(s32[128]{0:T(128)} %param.18) | copy-start | bytes 1540
  3.8 0.9 %copy-start.8 = (s32[128]{0:T(128)S(1)}, s32[128]{0:T(128)}, u32[]{:S(2)}) copy-start(s32[128]{0:T(128)} %param.20) | copy-start | bytes 1540
  3.8 0.9 %copy-start.9 = (f32[4]{0:T(128)S(1)}, f32[4]{0:T(128)}, u32[]{:S(2)}) copy-start(f32[4]{0:T(128)} %site_ref.1) | copy-start | bytes 52
  3.8 0.9 %copy-start.10 = (f32[128]{0:T(128)S(1)}, f32[128]{0:T(128)}, u32[]{:S(2)}) copy-start(f32[128]{0:T(128)} %param.31) | copy-start | bytes 1540
  3.8 0.9 %copy-start.11 = (f32[16]{0:T(128)S(1)}, f32[16]{0:T(128)}, u32[]{:S(2)}) copy-start(f32[16]{0:T(128)} %param.33) | copy-start | bytes 196
where the time goes:
time: 47.8 us; the launch traced here: 47.5 us
  Pallas kernels  39.9 us (83%)
  local copies, waits for them, and re-layouts  4.38 us (9%)
  between operations  3.19 us (7%)
    pallas_call x1, Pallas kernels, per_device(): pl.pallas_call(functools.partial(kernel, n_gx, n_gy), out_shape=(jax.Shap...  39.9 us
    unnamed x32, local copies, waits for them, and re-layouts  4.38 us

commit v1 on v0

--- a/solution.py
+++ b/solution.py
@@ -55,6 +55,27 @@
     return dot(a_high, b_high) + (dot(a_high, b_low) + dot(a_low, b_high))
 
 
+def terms3(x):
+    high = x.astype(bf16).astype(f32)
+    rest = x - high
+    middle = rest.astype(bf16).astype(f32)
+    return high, middle, rest - middle
+
+
+def sixfold(w):
+    high, middle, low = terms3(w)
+    return jnp.concatenate([high, high, middle, high, middle, low], 1).astype(bf16)
+
+
+def deep(left, x, full):
+    high, middle, low = terms3(x)
+    right = [high, middle, high]
+    if full:
+        right += [low, middle, high]
+    right = jnp.concatenate(right, 0).astype(bf16)
+    return dot(left[:, : right.shape[0]], right)
+
+
 def sub_iota(shape):
     return lax.broadcasted_iota(jnp.int32, shape, 0)
 
@@ -66,95 +87,122 @@
 def kernel(
     n_gx,
     n_gy,
-    pos_ref,
-    kind_ref,
-    neigh_ref,
-    count_ref,
-    live_ref,
-    send_ref,
-    embed_ref,
-    site_ref,
-    win_ref,
-    wmid_ref,
-    wout_ref,
-    contract_ref,
-    mix_ref,
-    skip_ref,
-    one_ref,
-    hidden_ref,
-    out_ref,
-    energy_ref,
-    forces_ref,
-    stress_ref,
-    packet,
-    table,
-    embed_pad,
-    place,
-    place_back,
-    pick,
-    rows,
-    grads,
-    sel,
-    rad0,
-    drad0,
-    rad1,
-    drad1,
-    feat0,
-    feat1,
-    deriv0,
-    deriv1,
-    mixed,
-    first,
-    gmix,
-    gfeat,
-    zed,
-    gown,
-    p_send,
-    p_recv,
-    f_send,
-    f_recv,
-    g_send,
-    g_recv,
-    q_send,
-    q_recv,
-    y_recv,
-    x_send,
-    x_recv,
-    p_ss,
-    p_rs,
-    f_ss,
-    f_rs,
-    g_ss,
-    g_rs,
-    q_ss,
-    q_rs,
-    y_ss,
-    y_rs,
-    x_ss,
-    x_rs,
+    *refs,
 ):
-    channels = embed_ref.shape[0]
-    kinds = embed_ref.shape[1]
+    ins = refs[:17]
+    (energy_ref, forces_ref, stress_ref) = refs[17:20]
+    (
+        pos_ref,
+        kind_ref,
+        neigh_ref,
+        count_ref,
+        live_ref,
+        send_ref,
+        embed_ref,
+        site_ref,
+        win_ref,
+        wmid_ref,
+        wout_ref,
+        contract_ref,
+        mix_ref,
+        skip_ref,
+        one_ref,
+        hidden_ref,
+        out_ref,
+    ) = refs[20:37]
+    (
+        packet,
+        table,
+        place,
+        place_back,
+        pick,
+        rows,
+        grads,
+        sel,
+        rad0,
+        drad0,
+        rad1,
+        drad1,
+        feat0,
+        feat1,
+        deriv0,
+        deriv1,
+        mixed,
+        first,
+        gmix,
+        gfeat,
+        zed,
+        gown,
+        p_send,
+        p_recv,
+        f_send,
+        f_recv,
+        g_send,
+        g_recv,
+        q_send,
+        q_recv,
+        mid6,
+        out6,
+        sums,
+        p_ss,
+        p_rs,
+        f_ss,
+        f_rs,
+        g_ss,
+        g_rs,
+        q_ss,
+        q_rs,
+        s_ss,
+        s_rs,
+        in_sem,
+    ) = refs[37:]
+    kinds, channels = embed_ref.shape
     slots, atoms = neigh_ref.shape
     edges = slots * atoms
     ghosts = send_ref.shape[1]
     ghost = ghosts // 8
-    basis_count = win_ref.shape[2]
-    hid = win_ref.shape[1]
+    basis_count, hid = win_ref.shape[1:]
     me_x = lax.axis_index("gx")
     me_y = lax.axis_index("gy")
 
+    n_dev = n_gx * n_gy
+
+    def wrapped(value, count):
+        return jnp.where(value >= count, value - count, value)
+
     def at(off_x, off_y):
         return {
-            "gx": lax.rem(me_x + (off_x + n_gx), n_gx),
-            "gy": lax.rem(me_y + (off_y + n_gy), n_gy),
+            "gx": wrapped(me_x + off_x % n_gx, n_gx),
+            "gy": wrapped(me_y + off_y % n_gy, n_gy),
         }
 
+    def peer(t, sign):
+        off_x, off_y = t // n_gy, t % n_gy
+        if sign < 0:
+            off_x, off_y = n_gx - off_x, n_gy - off_y
+        x, y = wrapped(me_x + off_x, n_gx), wrapped(me_y + off_y, n_gy)
+        return {"gx": x, "gy": y}, x * n_gy + y
+
+    def each_peer(act):
+        if n_dev <= 64:
+            for t in range(1, n_dev):
+                act(t)
+        else:
+            lax.fori_loop(1, n_dev, lambda t, carry: (act(t), carry)[1], 0)
+
     barrier = pltpu.get_barrier_semaphore()
-    friends = [(ox, oy) for ox, oy in directions if ox and oy]
-    friends += [(t, 0) for t in range(1, n_gx)] + [(0, t) for t in range(1, n_gy)]
-    for ox, oy in friends:
-        pl.semaphore_signal(barrier, inc=1, device_id=at(ox, oy), device_id_type=MESH)
+
+    def greet(t):
+        pl.semaphore_signal(barrier, inc=1, device_id=peer(t, 1)[0], device_id_type=MESH)
+
+    each_peer(greet)
+    vmem_refs = refs[20:37]
+    loads = [pltpu.make_async_copy(ins[i], vmem_refs[i], in_sem.at[i]) for i in range(17)]
+    early = (0, 1, 5)
+    for i in early + tuple(i for i in range(17) if i not in early):
+        loads[i].start()
+    for i in early:
+        loads[i].wait()
 
     kind = kind_ref[...]
     packet[...] = jnp.zeros_like(packet)
@@ -178,13 +226,16 @@
             device_id_type=MESH,
         )
 
-    pl.semaphore_wait(barrier, len(friends))
+    pl.semaphore_wait(barrier, n_dev - 1)
     p_copies = [
         ghost_copy(p_send.at[d // 2], p_recv.at[d], p_ss, p_rs, d, -1) for d in range(8)
     ]
     for copy in p_copies:
         copy.start()
 
+    for i in range(17):
+        if i not in early:
+            loads[i].wait()
     for k in range(slots):
         pick[:, k * atoms : (k + 1) * atoms] = (
             (sub_iota((atoms + ghosts, atoms)) == neigh_ref[k : k + 1, :])
@@ -197,26 +248,37 @@
         ).astype(bf16)
     table[...] = jnp.zeros_like(table)
     for layer in range(2):
-        for s in range(kinds):
-            base = (layer * kinds + s) * 8
-            table[base : base + 6, :] = contract_ref[layer, s]
-    table_high, table_low = halves(jnp.transpose(table[...]))
+        for p in range(6):
+            base = (layer * 6 + p) * 8
+            table[base : base + kinds, :] = contract_ref[layer, p]
+        table[104 + 8 * layer : 112 + 8 * layer, 0:hid] = win_ref[layer]
+    table[96 : 96 + kinds, :] = embed_ref[...]
+    turned_table = jnp.transpose(table[...])
+    table_terms = [term.astype(bf16) for term in terms3(turned_table)]
+    win6 = [
+        sixfold(turned_table[0:hid, 104 + 8 * l : 104 + 8 * l + basis_count]) for l in range(2)
+    ]
     for layer in range(2):
         for p in range(6):
             chosen = (
-                (sub_iota((channels, atoms)) == kind * 8 + (layer * kinds * 8 + p))
+                (sub_iota((channels, atoms)) == kind + (layer * 6 + p) * 8)
                 .astype(f32)
                 .astype(bf16)
             )
-            sel[layer, p] = dot(table_high, chosen) + dot(table_low, chosen)
-    embed_pad[...] = jnp.zeros_like(embed_pad)
-    embed_pad[:, 0:kinds] = embed_ref[...]
-    embed_stack = stacked(embed_pad[...], 2)
-    kind_local = (sub_iota((channels, atoms)) == kind).astype(f32).astype(bf16)
-    start_self = unstacked(dot(embed_stack, kind_local), channels, 2)
-    skip_part = dot3(skip_ref[0], start_self)
-    read_mix = dot3(hidden_ref[...], mix_ref[1])
-    read_skip = dot3(hidden_ref[...], skip_ref[1])
+            sel[layer, p] = sum(dot(term, chosen) for term in table_terms)
+        mid6[layer] = sixfold(wmid_ref[layer])
+        for b in range(wout_ref.shape[2] // channels):
+            part = slice(b * channels, (b + 1) * channels)
+            out6[layer, part, :] = sixfold(jnp.transpose(wout_ref[layer, :, part]))
+    embed_stack = stacked(turned_table, 3)
+    kind_local = (sub_iota((channels, atoms)) == kind + 96).astype(f32).astype(bf16)
+    start_self = unstacked(dot(embed_stack, kind_local), channels, 3)
+    skip_part = deep(sixfold(skip_ref[0]), start_self, True)
+    mix6 = sixfold(mix_ref[0])
+    hidden6 = sixfold(hidden_ref[...])
+    read_mix = deep(hidden6, mix_ref[1], True)
+    read_skip = deep(hidden6, skip_ref[1], True)
+    read_mix6, read_skip6 = sixfold(read_mix), sixfold(read_skip)
     live = (lane_iota((1, atoms)) < live_ref[0]).astype(f32)
     one_full = jnp.transpose(jnp.broadcast_to(one_ref[...], (atoms, channels)))
     readers = hidden_ref.shape[0]
@@ -243,9 +305,9 @@
     ext = stacked(jnp.concatenate(tiles, 1), 3)
     rows[0:8, :] = unstacked(dot(ext, pick[...]), 8, 3)
     kind_edge = (
-        (sub_iota((channels, edges)).astype(f32) == rows[3:4, :]).astype(f32).astype(bf16)
+        ((sub_iota((channels, edges)) - 96).astype(f32) == rows[3:4, :]).astype(f32).astype(bf16)
     )
-    feat0[...] = unstacked(dot(embed_stack, kind_edge), channels, 2)
+    feat0[...] = unstacked(dot(embed_stack, kind_edge), channels, 3)
     for k in range(slots):
         lanes = slice(k * atoms, (k + 1) * atoms)
         x = rows[0:1, lanes] - pos_ref[0:1, :]
@@ -268,27 +330,23 @@
     scaled = jnp.broadcast_to(rows[8:9, :], (basis_count, edges))
     gap = (scaled - sub_iota((basis_count, edges)).astype(f32) * spacing) / spacing
     basis = jnp.exp(-0.5 * gap * gap)
-    basis_all = jnp.concatenate([basis, basis * gap * (-1.0 / spacing)], 1)
-
-    def deep(w, x):
-        w_high, w_low = halves(w)
-        w_high, w_low = w_high.astype(f32), w_low.astype(f32)
-        x_high = x.astype(bf16).astype(f32)
-        left = jnp.concatenate([w_high, w_high, w_low], 1).astype(bf16)
-        right = jnp.concatenate([x_high, x - x_high, x_high], 0).astype(bf16)
-        return dot(left, right)
-
-    def silu_pair(z):
-        value, slope = z[:, :edges], z[:, edges:]
-        gate = 1.0 / (1.0 + jnp.exp(-value))
-        act = value * gate
-        return act, (gate + act * (1.0 - gate)) * slope
-
-    def network(layer):
-        h, dh = silu_pair(deep(win_ref[layer], basis_all))
-        h, dh = silu_pair(deep(wmid_ref[layer], jnp.concatenate([h, dh], 1)))
-        env = rows[9:10, :]
-        return h * env, (dh - h) * env
+
+    env = rows[9:10, :]
+
+    def values(layer):
+        act, gains = basis, []
+        for left in (win6[layer], mid6[layer]):
+            value = deep(left, act, True)
+            gate = 1.0 / (1.0 + jnp.exp(-value))
+            act = value * gate
+            gains.append(gate + act * (1.0 - gate))
+        act = act * env
+        return act, gains
+
+    def slopes(layer, act, gains):
+        slope = gains[0] * deep(win6[layer], basis * gap * (-1.0 / spacing), False)
+        slope = gains[1] * deep(mid6[layer], slope, False)
+        return slope * env - act
 
     def moments(layer, rad, feat, deriv):
         def step(block, carry):
@@ -328,12 +386,11 @@
 
         lax.fori_loop(0, channels // BLOCK, step, 0)
 
-    act0, slope0 = network(0)
-    rad0[...] = deep(wout_ref[0], act0)
+    act0, gains0 = values(0)
+    rad0[...] = deep(out6[0], act0, True)
     moments(0, rad0, feat0, deriv0)
-    first[...] = dot3(mix_ref[0], mixed[...]) + skip_part
-    first_high, first_low = halves(first[...])
-    sent_first = dot_nt(place_back[...], first_high) + dot_nt(place_back[...], first_low)
+    first[...] = deep(mix6, mixed[...], True) + skip_part
+    sent_first = sum(dot_nt(place_back[...], term.astype(bf16)) for term in terms3(first[...]))
     for d in range(8):
         f_send[d] = sent_first[d * ghost : (d + 1) * ghost]
     f_copies = [ghost_copy(f_send.at[d], f_recv.at[d], f_ss, f_rs, d, -1) for d in range(8)]
@@ -342,10 +399,10 @@
     for copy in p_copies:
         copy.wait_send()
 
-    act1, slope1 = network(1)
-    rad1[...] = deep(wout_ref[1], act1)
-    drad0[...] = deep(wout_ref[0], slope0)
-    drad1[...] = deep(wout_ref[1], slope1)
+    act1, gains1 = values(1)
+    rad1[...] = deep(out6[1], act1, True)
+    drad1[...] = deep(out6[1], slopes(1, act1, gains1), False)
+    drad0[...] = deep(out6[0], slopes(0, act0, gains0), False)
 
     for copy in f_copies:
         copy.wait_recv()
@@ -353,10 +410,10 @@
     turned = [first[...]] + [
         jnp.transpose(arrived[b * atoms : (b + 1) * atoms]) for b in range(ghosts // atoms)
     ]
-    ext_first = stacked(jnp.concatenate(turned, 1), 2)
-    feat1[...] = unstacked(dot(ext_first, pick[...]), channels, 2)
+    ext_first = stacked(jnp.concatenate(turned, 1), 3)
+    feat1[...] = unstacked(dot(ext_first, pick[...]), channels, 3)
     moments(1, rad1, feat1, deriv1)
-    inner = dot3(read_mix, mixed[...]) + dot3(read_skip, first[...])
+    inner = deep(read_mix6, mixed[...], True) + deep(read_skip6, first[...], True)
     gate = 1.0 / (1.0 + jnp.exp(-inner))
     act = inner * gate
     g_inner = (gate + act * (1.0 - gate)) * out_column * live
@@ -396,7 +453,7 @@
     energy_lanes = live * jnp.sum(one_full * first[...], axis=0, keepdims=True)
     energy_lanes = energy_lanes + live * jnp.sum(out_column * act, axis=0, keepdims=True)
     for s in range(kinds):
-        energy_lanes = energy_lanes + jnp.where(kind == s, site_ref[s], 0.0) * live
+        energy_lanes = energy_lanes + jnp.where(kind == s, site_ref[0:1, s : s + 1], 0.0) * live
 
     def edge_terms(rad, drad, feat, deriv, base, lanes):
         here = pl.ds(base, BLOCK)
@@ -437,9 +494,9 @@
             return tuple(carry[i] + g * terms[i] for i in range(3))
 
         zero = jnp.zeros((BLOCK, atoms), f32)
-        sums = lax.fori_loop(0, channels // BLOCK, second_terms, (zero, zero, zero))
+        found = lax.fori_loop(0, channels // BLOCK, second_terms, (zero, zero, zero))
         for i in range(3):
-            grads[i : i + 1, lanes] = jnp.sum(sums[i], axis=0, keepdims=True)
+            grads[i : i + 1, lanes] = jnp.sum(found[i], axis=0, keepdims=True)
 
     for copy in g_copies:
         copy.wait_recv()
@@ -479,50 +536,28 @@
                 total = total + rows[a : a + 1, lanes] * grads[b : b + 1, lanes]
             partial.append(total)
     partial.append(jnp.zeros((5, atoms), f32))
-    y_recv[me_y] = jnp.concatenate(partial, 0)
-
-    def line_copies(buf, ss, rs, me, count, where):
-        outgoing = []
-        incoming = []
-        for t in range(1, count):
-            source = lax.rem(me + (count - t), count)
-            outgoing.append(
-                pltpu.make_async_remote_copy(
-                    src_ref=buf.at[me],
-                    dst_ref=buf.at[me],
-                    send_sem=ss.at[t],
-                    recv_sem=rs.at[t],
-                    device_id=where(t),
-                    device_id_type=MESH,
-                )
-            )
-            incoming.append(
-                pltpu.make_async_remote_copy(
-                    src_ref=buf.at[source],
-                    dst_ref=buf.at[source],
-                    send_sem=ss.at[t],
-                    recv_sem=rs.at[t],
-                    device_id=where(t),
-                    device_id_type=MESH,
-                )
-            )
-        return outgoing, incoming
-
-    y_out, y_in = line_copies(y_recv, y_ss, y_rs, me_y, n_gy, lambda t: at(0, t))
-    for copy in y_out:
-        copy.start()
+    column = jnp.sum(jnp.concatenate(partial, 0), axis=1, keepdims=True)
+    mine = me_x * n_gy + me_y
+    sums[mine] = jnp.sum(
+        jnp.where(sub_iota((16, atoms)) == lane_iota((16, atoms)), column, 0.0),
+        axis=0,
+        keepdims=True,
+    )
+
+    def sum_copy(t, slot):
+        return pltpu.make_async_remote_copy(
+            src_ref=sums.at[slot],
+            dst_ref=sums.at[slot],
+            send_sem=s_ss.at[t],
+            recv_sem=s_rs.at[t],
+            device_id=peer(t, 1)[0],
+            device_id_type=MESH,
+        )
+
+    each_peer(lambda t: sum_copy(t, mine).start())
     own_grad = ext_grad[:, :atoms]
     for k in range(slots):
         own_grad = own_grad - grads[:, k * atoms : (k + 1) * atoms]
-    for copy in y_in:
-        copy.wait_recv()
-    total = y_recv[0]
-    for t in range(1, n_gy):
-        total = total + y_recv[t]
-    x_recv[me_x] = total
-    x_out, x_in = line_copies(x_recv, x_ss, x_rs, me_x, n_gx, lambda t: at(t, 0))
-    for copy in x_out:
-        copy.start()
 
     for copy in q_copies:
         copy.wait_recv()
@@ -532,23 +567,15 @@
     home_pos = unstacked(dot(stacked(jnp.concatenate(tiles, 1), 2), place_back[...]), 8, 2)
     forces_ref[...] = -(own_grad + home_pos)[0:3]
 
-    for copy in x_in:
-        copy.wait_recv()
-    total = x_recv[0]
-    for t in range(1, n_gx):
-        total = total + x_recv[t]
-    total = jnp.sum(total, axis=1, keepdims=True)
-    scaled_total = total / total[1:2]
-    energy_ref[...] = scaled_total[0:1]
-    corner_r, corner_c = sub_iota((3, 3)), lane_iota((3, 3))
-    stress = jnp.zeros((3, 3), f32)
+    each_peer(lambda t: sum_copy(t, peer(t, -1)[1]).wait_recv())
+    total = jnp.sum(sums[...], axis=0)
+    total = total / total[:, 1:2]
+    energy_ref[...] = total[:, 0:1]
     for a in range(3):
-        for b in range(3):
-            value = scaled_total[2 + 3 * a + b : 3 + 3 * a + b]
-            stress = jnp.where((corner_r == a) & (corner_c == b), value, stress)
-    stress_ref[...] = stress
-    for copy in q_copies + y_out + x_out:
+        stress_ref[a : a + 1, :] = total[:, 2 + 3 * a : 5 + 3 * a]
+    for copy in q_copies:
         copy.wait_send()
+    each_peer(lambda t: sum_copy(t, mine).wait_send())
 
 
 def solution(mesh):
@@ -558,18 +585,24 @@
         positions, species, neighbours, counts, live_atoms, ghost_send, embed, site_energy,
         radial_in, radial_mid, radial_out, contract, mix, skip, read_one, read_hidden, read_out,
     ):
-        channels = embed.shape[0]
+        channels, hid = embed.shape[0], radial_mid.shape[1]
         slots, atoms = neighbours.shape
         edges = slots * atoms
         ghosts = ghost_send.shape[0]
         ghost = ghosts // 8
         vmem = pl.BlockSpec(memory_space=pltpu.VMEM)
-        smem = pl.BlockSpec(memory_space=pltpu.SMEM)
         sems = pltpu.SemaphoreType.DMA
         wide = (channels, edges)
-        scratch = [
+        operands = (
+            positions, species[None], neighbours, counts[None], live_atoms,
+            ghost_send[None], embed.T, site_energy[None], jnp.swapaxes(radial_in, 1, 2),
+            radial_mid, jnp.swapaxes(radial_out, 1, 2), jnp.swapaxes(contract, 1, 2),
+            mix, skip, read_one[None], read_hidden, read_out[None],
+        )
+        scratch = [pltpu.VMEM(x.shape, x.dtype) for x in operands]
+        scratch[4] = pltpu.SMEM(live_atoms.shape, live_atoms.dtype)
+        scratch += [
             pltpu.VMEM((8, atoms), f32),
-            pltpu.VMEM((channels, channels), f32),
             pltpu.VMEM((channels, channels), f32),
             pltpu.VMEM((atoms, ghosts), bf16),
             pltpu.VMEM((ghosts, atoms), bf16),
@@ -599,11 +632,11 @@
             pltpu.VMEM((8, ghost, channels), f32),
             pltpu.VMEM((4, 8, 2 * ghost), f32),
             pltpu.VMEM((8, 8, 2 * ghost), f32),
-            pltpu.VMEM((n_gy, 16, atoms), f32),
-            pltpu.VMEM((16, atoms), f32),
-            pltpu.VMEM((n_gx, 16, atoms), f32),
+            pltpu.VMEM((2, hid, 6 * hid), bf16),
+            pltpu.VMEM((2, 3 * channels, 6 * hid), bf16),
+            pltpu.VMEM((n_gx * n_gy, 1, atoms), f32),
         ]
-        scratch += [sems((8,))] * 8 + [sems((n_gy,))] * 2 + [sems((n_gx,))] * 2
+        scratch += [sems((8,))] * 8 + [sems((n_gx * n_gy,))] * 2 + [sems((17,))]
         energy, forces, stress = pl.pallas_call(
             functools.partial(kernel, n_gx, n_gy),
             out_shape=(
@@ -611,17 +644,13 @@
                 jax.ShapeDtypeStruct((3, atoms), f32),
                 jax.ShapeDtypeStruct((3, 3), f32),
             ),
-            in_specs=[vmem] * 4 + [smem] + [vmem] * 2 + [smem] + [vmem] * 9,
+            in_specs=[pl.BlockSpec(memory_space=pltpu.HBM)] * 17,
             out_specs=(vmem, vmem, vmem),
             scratch_shapes=scratch,
             compiler_params=pltpu.CompilerParams(
-                collective_id=0, has_side_effects=True, vmem_limit_bytes=50 * 1024 * 1024
+                collective_id=0, has_side_effects=True, vmem_limit_bytes=67018752
             ),
-        )(
-            positions, species[None], neighbours, counts[None], live_atoms, ghost_send[None],
-            embed, site_energy, radial_in, radial_mid, radial_out, contract, mix, skip,
-            read_one[None], read_hidden, read_out[None],
-        )
+        )(*operands)
         return energy.reshape(()), forces, stress
 
     flat = P(("gx", "gy"))

time: 47.8 us -> 42.7 us (0.89)
  local copies, waits for them, and re-layouts: 4.38 us -> 1.27 us
  Pallas kernels: 39.9 us -> 38.1 us
    unnamed x32 -> x6, local copies, waits for them, and re-layouts: 4.38 us -> 1.27 us
    pallas_call x1, Pallas kernels: 39.9 us -> 38.1 us  [per_device(): pl.pallas_call(functools.partial(kernel, n_gx, n_gy), out_shape=(jax.Shap...]
where the time goes in v1:
time: 42.7 us; the launch traced here: 42.4 us
  Pallas kernels  38.1 us (89%)
  between operations  3.05 us (7%)
  local copies, waits for them, and re-layouts  1.27 us (3%)
    pallas_call x1, Pallas kernels, per_device(): pl.pallas_call(functools.partial(kernel, n_gx, n_gy), out_shape=(jax.Shap...  38.1 us
    unnamed x6, local copies, waits for them, and re-layouts  1.27 us

profile of v1, /device:TPU:0, one launch (start us, length us, event | category | flops | bytes accessed | tf_op | source)
XLA Modules:
  0.0 42.4 jit_solution(3125870342523499710)
XLA Ops:
  1.3 38.1 %shard_map.184 = (f32[1,1]{1,0:T(1,128)}, f32[3,128]{1,0:T(4,128)}, f32[3,3]{1,0:T(4,128)}) custom-call(f32[3,128]{1,0:T(4,128)} %refs_0_.1, s32[1,128]{1,0:T(1,128)} %bitcast.16, s32[8,128]{1,0:T(8,128)} %refs_2_.1, s32[1,128]{1,0:T(1,128)} %bitcast.17, s32[1]{0:T(128)S(6)} %copy.23.refs_4_, s32[1,512]{1,0:T(1,128)} %bitcast.14, f32[4,128]{1,0:T(4,128)} %bitcast.15, ...), custom_call_target="tpu_custom_call" | custom-call | tf_op jit(solution)/shard_map/pallas_call | solution.py:640
  39.4 0.0 copy-start.1
  40.0 0.0 copy-done.1
  40.1 0.0 copy-start
  40.1 0.6 %copy.25 = f32[3,128]{1,0:T(4,128)} copy(f32[3,128]{1,0:T(4,128)S(1)} %copy-done.1) | data formatting | bytes 3072
  40.7 0.1 copy-done
  40.7 0.6 %copy.26 = f32[3,3]{1,0:T(4,128)} copy(f32[3,3]{1,0:T(4,128)S(1)} %copy-done) | data formatting | bytes 72
Async XLA Ops:
  39.4 0.7 %copy-start.1 = (f32[3,128]{1,0:T(4,128)S(1)}, f32[3,128]{1,0:T(4,128)}, u32[]{:S(2)}) copy-start(f32[3,128]{1,0:T(4,128)} %get-tuple-element.13) | copy-start | bytes 4612
  40.1 0.7 %copy-start = (f32[3,3]{1,0:T(4,128)S(1)}, f32[3,3]{1,0:T(4,128)}, u32[]{:S(2)}) copy-start(f32[3,3]{1,0:T(4,128)} %get-tuple-element.14) | copy-start | bytes 112

commit v2 on v1

--- a/solution.py
+++ b/solution.py
@@ -404,57 +404,6 @@
     drad1[...] = deep(out6[1], slopes(1, act1, gains1), False)
     drad0[...] = deep(out6[0], slopes(0, act0, gains0), False)
 
-    for copy in f_copies:
-        copy.wait_recv()
-    arrived = f_recv[...].reshape(ghosts, channels)
-    turned = [first[...]] + [
-        jnp.transpose(arrived[b * atoms : (b + 1) * atoms]) for b in range(ghosts // atoms)
-    ]
-    ext_first = stacked(jnp.concatenate(turned, 1), 3)
-    feat1[...] = unstacked(dot(ext_first, pick[...]), channels, 3)
-    moments(1, rad1, feat1, deriv1)
-    inner = deep(read_mix6, mixed[...], True) + deep(read_skip6, first[...], True)
-    gate = 1.0 / (1.0 + jnp.exp(-inner))
-    act = inner * gate
-    g_inner = (gate + act * (1.0 - gate)) * out_column * live
-    gmix[...] = dot3(jnp.transpose(read_mix), g_inner)
-
-    def feature_grad(block, carry):
-        base = pl.multiple_of(block * BLOCK, BLOCK)
-        here = pl.ds(base, BLOCK)
-        g = gmix[here, :]
-        ga = [g * deriv1[m, here, :] for m in range(9)]
-        for k in range(slots):
-            lanes = slice(k * atoms, (k + 1) * atoms)
-            t1 = sum(ga[1 + m] * rows[m : m + 1, lanes] for m in range(3))
-            t2 = sum(ga[4 + m] * rows[3 + m : 4 + m, lanes] for m in range(5))
-            total = ga[0] * rad1[pl.ds(base, BLOCK), lanes]
-            total = total + t1 * rad1[pl.ds(base + channels, BLOCK), lanes]
-            total = total + t2 * rad1[pl.ds(base + 2 * channels, BLOCK), lanes]
-            high = total.astype(bf16)
-            gfeat[pl.ds(base, BLOCK), lanes] = high
-            gfeat[pl.ds(base + channels, BLOCK), lanes] = (total - high.astype(f32)).astype(bf16)
-        return carry
-
-    lax.fori_loop(0, channels // BLOCK, feature_grad, 0)
-    back = dot_nt(pick[atoms : atoms + ghosts, :], gfeat[...])
-    back = back[:, :channels] + back[:, channels:]
-    for d in range(8):
-        g_send[d] = back[d * ghost : (d + 1) * ghost]
-    g_copies = [ghost_copy(g_send.at[d], g_recv.at[d], g_ss, g_rs, d, 1) for d in range(8)]
-    for copy in g_copies:
-        copy.start()
-    for copy in f_copies:
-        copy.wait_send()
-
-    own_back = dot_nt(pick[0:atoms, :], gfeat[...])
-    own_back = jnp.transpose(own_back[:, :channels] + own_back[:, channels:])
-    gown[...] = own_back + dot3(jnp.transpose(read_skip), g_inner) + one_full * live
-    energy_lanes = live * jnp.sum(one_full * first[...], axis=0, keepdims=True)
-    energy_lanes = energy_lanes + live * jnp.sum(out_column * act, axis=0, keepdims=True)
-    for s in range(kinds):
-        energy_lanes = energy_lanes + jnp.where(kind == s, site_ref[0:1, s : s + 1], 0.0) * live
-
     def edge_terms(rad, drad, feat, deriv, base, lanes):
         here = pl.ds(base, BLOCK)
         x, y, z = [rows[m : m + 1, lanes] for m in range(3)]
@@ -484,6 +433,58 @@
         return carry
 
     lax.fori_loop(0, channels // BLOCK, first_terms, 0)
+
+    for copy in f_copies:
+        copy.wait_recv()
+    arrived = f_recv[...].reshape(ghosts, channels)
+    turned = [first[...]] + [
+        jnp.transpose(arrived[b * atoms : (b + 1) * atoms]) for b in range(ghosts // atoms)
+    ]
+    ext_first = stacked(jnp.concatenate(turned, 1), 3)
+    feat1[...] = unstacked(dot(ext_first, pick[...]), channels, 3)
+    moments(1, rad1, feat1, deriv1)
+    inner = deep(read_mix6, mixed[...], True) + deep(read_skip6, first[...], True)
+    gate = 1.0 / (1.0 + jnp.exp(-inner))
+    act = inner * gate
+    g_inner = (gate + act * (1.0 - gate)) * out_column * live
+    gmix[...] = dot3(jnp.transpose(read_mix), g_inner)
+
+    def feature_grad(block, carry):
+        base = pl.multiple_of(block * BLOCK, BLOCK)
+        here = pl.ds(base, BLOCK)
+        g = gmix[here, :]
+        ga = [g * deriv1[m, here, :] for m in range(9)]
+        for k in range(slots):
+            lanes = slice(k * atoms, (k + 1) * atoms)
+            t1 = sum(ga[1 + m] * rows[m : m + 1, lanes] for m in range(3))
+            t2 = sum(ga[4 + m] * rows[3 + m : 4 + m, lanes] for m in range(5))
+            total = ga[0] * rad1[pl.ds(base, BLOCK), lanes]
+            total = total + t1 * rad1[pl.ds(base + channels, BLOCK), lanes]
+            total = total + t2 * rad1[pl.ds(base + 2 * channels, BLOCK), lanes]
+            high = total.astype(bf16)
+            gfeat[pl.ds(base, BLOCK), lanes] = high
+            gfeat[pl.ds(base + channels, BLOCK), lanes] = (total - high.astype(f32)).astype(bf16)
+        return carry
+
+    lax.fori_loop(0, channels // BLOCK, feature_grad, 0)
+    back = dot_nt(pick[atoms : atoms + ghosts, :], gfeat[...])
+    back = back[:, :channels] + back[:, channels:]
+    for d in range(8):
+        g_send[d] = back[d * ghost : (d + 1) * ghost]
+    g_copies = [ghost_copy(g_send.at[d], g_recv.at[d], g_ss, g_rs, d, 1) for d in range(8)]
+    for copy in g_copies:
+        copy.start()
+    for copy in f_copies:
+        copy.wait_send()
+
+    own_back = dot_nt(pick[0:atoms, :], gfeat[...])
+    own_back = jnp.transpose(own_back[:, :channels] + own_back[:, channels:])
+    gown[...] = own_back + dot3(jnp.transpose(read_skip), g_inner) + one_full * live
+    energy_lanes = live * jnp.sum(one_full * first[...], axis=0, keepdims=True)
+    energy_lanes = energy_lanes + live * jnp.sum(out_column * act, axis=0, keepdims=True)
+    for s in range(kinds):
+        energy_lanes = energy_lanes + jnp.where(kind == s, site_ref[0:1, s : s + 1], 0.0) * live
+
     for k in range(slots):
         lanes = slice(k * atoms, (k + 1) * atoms)
 

time: 42.7 us -> 42.7 us (level)
  no operation moved by 1% of the time
where the time goes in v2:
time: 42.7 us; the launch traced here: 42.4 us
  Pallas kernels  38.1 us (89%)
  between operations  3.05 us (7%)
  local copies, waits for them, and re-layouts  1.27 us (3%)
    pallas_call x1, Pallas kernels, per_device(): pl.pallas_call(functools.partial(kernel, n_gx, n_gy), out_shape=(jax.Shap...  38.1 us
    unnamed x6, local copies, waits for them, and re-layouts  1.27 us

profile of v2, /device:TPU:0, one launch (start us, length us, event | category | flops | bytes accessed | tf_op | source)
XLA Modules:
  0.0 42.4 jit_solution(14571356850789105109)
XLA Ops:
  1.3 38.1 %shard_map.184 = (f32[1,1]{1,0:T(1,128)}, f32[3,128]{1,0:T(4,128)}, f32[3,3]{1,0:T(4,128)}) custom-call(f32[3,128]{1,0:T(4,128)} %refs_0_.1, s32[1,128]{1,0:T(1,128)} %bitcast.16, s32[8,128]{1,0:T(8,128)} %refs_2_.1, s32[1,128]{1,0:T(1,128)} %bitcast.17, s32[1]{0:T(128)S(6)} %copy.23.refs_4_, s32[1,512]{1,0:T(1,128)} %bitcast.14, f32[4,128]{1,0:T(4,128)} %bitcast.15, ...), custom_call_target="tpu_custom_call" | custom-call | tf_op jit(solution)/shard_map/pallas_call | solution.py:641
  39.4 0.0 copy-start.1
  40.0 0.0 copy-done.1
  40.1 0.0 copy-start
  40.1 0.6 %copy.25 = f32[3,128]{1,0:T(4,128)} copy(f32[3,128]{1,0:T(4,128)S(1)} %copy-done.1) | data formatting | bytes 3072
  40.7 0.1 copy-done
  40.7 0.6 %copy.26 = f32[3,3]{1,0:T(4,128)} copy(f32[3,3]{1,0:T(4,128)S(1)} %copy-done) | data formatting | bytes 72
Async XLA Ops:
  39.4 0.7 %copy-start.1 = (f32[3,128]{1,0:T(4,128)S(1)}, f32[3,128]{1,0:T(4,128)}, u32[]{:S(2)}) copy-start(f32[3,128]{1,0:T(4,128)} %get-tuple-element.13) | copy-start | bytes 4612
  40.1 0.7 %copy-start = (f32[3,3]{1,0:T(4,128)S(1)}, f32[3,3]{1,0:T(4,128)}, u32[]{:S(2)}) copy-start(f32[3,3]{1,0:T(4,128)} %get-tuple-element.14) | copy-start | bytes 112
